TPU v7x, 32 devices: a whole 2x2x4 slice. The times are simulated.
32 devices in a mesh: gx: 4 (over x, core), gy: 2 (over y), gz: 4 (over z).
Axes of the slice: x: 2, y: 2, z: 4, core: 2. Of those that a mesh axis runs over, the one named last changes fastest.
Arguments:
- velocity: float32 [3, 128, 192, 1024], P(None, 'gx', 'gy', 'gz'), may hold values from -6 to 6
Outputs:
- magnitude: float32 [128, 192, 1024], P('gx', ('gy', 'gz'))
- level_one: float32 [64, 96, 512], P('gx', 'gy')
- level_two: float32 [32, 48, 256], P('gx', 'gy')
- level_three: float32 [16, 24, 128], P('gx', 'gy')
- level_four: float32 [8, 12, 64], P('gx', 'gy')
- level_five: float32 [4, 6, 32], P('gx', 'gy')
All inputs are finite; a program needn't handle non-finite values.
Results may differ from a plain program's by a relative error of at most 0.000075.
Values sent between devices are 32-bit elements; how exact they have to be, the bound alone decides.
A program may use at most 256 MiB of HBM per device.

v0:
```python
import functools

import jax
import jax.numpy as jnp
from jax import lax
from jax.experimental import pallas as pl
from jax.experimental.pallas import tpu as pltpu
from jax.sharding import PartitionSpec as P

MESH = pl.DeviceIdType.MESH
LANES = 128
CHUNKS = 4
ORDER = (1, 2, 3, 0)
LOAD_ORDER = (1, 2, 0, 3)
MIB = 1024 * 1024


def remote(src, dst, send, recv, device):
    return pltpu.make_async_remote_copy(
        src_ref=src, dst_ref=dst, send_sem=send, recv_sem=recv, device_id=device, device_id_type=MESH
    )


def halve_lanes(rows):
    depth = rows.shape[1]
    fine = lax.broadcasted_iota(jnp.int32, (depth, depth // 2), 0)
    coarse = lax.broadcasted_iota(jnp.int32, (depth, depth // 2), 1)
    weight = jnp.where(fine // 2 == coarse, 0.125, 0.0).astype(jnp.bfloat16)
    high = rows.astype(jnp.bfloat16)
    rest = rows - high.astype(jnp.float32)
    low = rest.astype(jnp.bfloat16)
    last = (rest - low.astype(jnp.float32)).astype(jnp.bfloat16)

    def dot(a):
        return jnp.dot(a, weight, preferred_element_type=jnp.float32)

    return dot(high) + (dot(low) + dot(last))


def pooled(read, count, size, work):
    tiles = work.shape[0]
    for i in range(count):
        value = read(2 * i) + read(2 * i + 1)
        depth = value.shape[1]
        for t in range(tiles):
            wide = min(LANES, depth - t * LANES)
            work[t, i * size:(i + 1) * size, :wide] = value[:, t * LANES:t * LANES + wide]
    lines = count * size // 2
    parts = [
        work[t, pl.ds(0, lines, stride=2), :] + work[t, pl.ds(1, lines, stride=2), :] for t in range(tiles)]
    return halve_lanes(jnp.concatenate(parts, axis=1)[:, :depth])


def carries(n, j, up, q, s):
    low, high = min(q, s), max(q, s)
    if up:
        return j < n - 1 and (high <= j or (low <= j and high > j + 1 and 2 * (j + 1) < n))
    return j > 0 and (low >= j or (high >= j and low < j - 1 and 2 * (j - 1) >= n))


def blocks(n):
    return [(q, s) for q in range(n) for s in range(n)]


def mag_time(n, s, q, k):
    d = abs(s - q)
    if s in (0, n - 1):
        return 4 * (k + 1) if d == 1 else 20 + 14 * (k + (d - 1) / (n - 2))
    outward = q < s if 2 * s < n else q > s
    return 4 * k + 6 if outward else 12 * (k + d / n)


def events(n, me):
    @functools.lru_cache(None)
    def ready(j, q, s, k):
        if j == s:
            return 0.0
        if j == q:
            return mag_time(n, s, q, k)
        for i, up in ((j - 1, True), (j + 1, False)):
            if 0 <= i < n and carries(n, i, up, q, s):
                crossing = 2 * (i + 1) == n if up else 2 * i == n
                return max(ready(i, q, s, k), (50 if crossing else 20) + 2 * k) + 3
        raise ValueError((j, q, s))

    found = []
    for k in range(CHUNKS):
        for q, s in blocks(n):
            if s != me:
                found.append((ready(me, q, s, k), q, s, k))
    return sorted(found)


def kernel(
    sizes, vel_hbm, pencil, one,
    vel, ypack, yhalo, zpack, zhalo, zside, stage, piece, work,
    load_sem, xs_sem, xr_sem, ys_sem, yr_sem, zs_sem, zr_sem, as_sem, ar_sem, move_sem, piece_sem,
):
    nx, ny, nz = sizes
    gx, gy, me = lax.axis_index("gx"), lax.axis_index("gy"), lax.axis_index("gz")
    _, planes, cols, depth = vel_hbm.shape
    rows = cols // nz
    half = depth // 2
    step = planes // CHUNKS
    pairs = step // 2
    group = pairs * rows // 2
    f32 = jnp.float32

    def at(dx=0, dy=0, dz=0):
        return (lax.rem(gx + dx + nx, nx), lax.rem(gy + dy + ny, ny), lax.rem(me + dz + nz, nz))

    barrier = pltpu.get_barrier_semaphore()
    friends = [at(dx=1), at(dx=-1), at(dy=1), at(dy=-1)] + [at(dz=d) for d in range(1, nz)]
    for friend in friends:
        pl.semaphore_signal(barrier, inc=1, device_id=friend, device_id_type=MESH)

    loads = {}
    for k in LOAD_ORDER:
        loads[k] = pltpu.make_async_copy(
            vel_hbm.at[:, pl.ds(k * step, step)], vel.at[:, pl.ds(1 + k * step, step)], load_sem.at[k])
        loads[k].start()
    pl.semaphore_wait(barrier, len(friends))

    xcopies = [
        remote(vel_hbm.at[pl.ds(1, 2), planes - 1], vel.at[pl.ds(1, 2), 0], xs_sem.at[0], xr_sem.at[0], at(dx=1)),
        remote(vel_hbm.at[pl.ds(1, 2), 0], vel.at[pl.ds(1, 2), planes + 1], xs_sem.at[1], xr_sem.at[1], at(dx=-1)),
    ]
    for copy in xcopies:
        copy.start()

    lane = lax.broadcasted_iota(jnp.int32, (cols, LANES), 1)
    sides = {}
    for k in ORDER:
        def pack(i, carry):
            first, last = carry
            x = k * step + i
            for c in range(2):
                first = jnp.where(lane == c * step + i, vel[c, x + 1, :, 0:1], first)
                last = jnp.where(lane == c * step + i, vel[c, x + 1, :, depth - 1:depth], last)
                ypack[0, c, pl.ds(x, 1), :] = vel[2 * c, x + 1, 0:1, :]
                ypack[1, c, pl.ds(x, 1), :] = vel[2 * c, x + 1, cols - 1:cols, :]
            return first, last

        loads[k].wait()
        zero = jnp.zeros((cols, LANES), f32)
        ends = lax.fori_loop(0, step, pack, (zero, zero))
        fill = jnp.zeros((LANES - cols, LANES), f32)
        for e in range(2):
            zpack[e, k] = jnp.concatenate([ends[e], fill], axis=0).T[:2 * step]
        mine = pl.ds(k * step, step)
        sides[k] = [
            remote(ypack.at[1, :, mine], yhalo.at[0, :, mine], ys_sem.at[0, k], yr_sem.at[0, k], at(dy=1)),
            remote(ypack.at[0, :, mine], yhalo.at[1, :, mine], ys_sem.at[1, k], yr_sem.at[1, k], at(dy=-1)),
            remote(zpack.at[1, k], zhalo.at[0, k], zs_sem.at[0, k], zr_sem.at[0, k], at(dz=1)),
            remote(zpack.at[0, k], zhalo.at[1, k], zs_sem.at[1, k], zr_sem.at[1, k], at(dz=-1)),
        ]
        for copy in sides[k]:
            copy.start()

    row = lax.broadcasted_iota(jnp.int32, (cols, depth), 0)
    deep = lax.broadcasted_iota(jnp.int32, (cols, depth), 1)

    def second(c, x):
        field = vel[2 * c, x + 1]
        ahead = jnp.where(row == cols - 1, yhalo[1, c, pl.ds(x, 1), :], pltpu.roll(field, cols - 1, 0))
        behind = jnp.where(row == 0, yhalo[0, c, pl.ds(x, 1), :], pltpu.roll(field, 1, 0))
        return ahead - behind

    def third(c, x, i):
        field = vel[c, x + 1]
        here = c * step + i
        after = pltpu.roll(zside[1], LANES - 1 - here, 1)
        before = pltpu.roll(zside[0], lax.rem(LANES - here, LANES), 1)
        after, before = (jnp.concatenate([a] * (depth // LANES), axis=1) for a in (after, before))
        ahead = jnp.where(deep == depth - 1, after, pltpu.roll(field, depth - 1, 1))
        behind = jnp.where(deep == 0, before, pltpu.roll(field, 1, 1))
        return ahead - behind

    def magnitude(x, i):
        total = second(1, x) - third(1, x, i)
        total = total * total
        part = third(0, x, i) - (vel[2, x + 2] - vel[2, x])
        total = total + part * part
        part = (vel[1, x + 2] - vel[1, x]) - second(0, x)
        total = total + part * part
        return jnp.sqrt(1.0 + 0.25 * total)

    def block(target, first, count, k):
        here = pl.ds(pl.multiple_of(me * depth, LANES), depth)
        return remote(
            stage.at[target, pl.ds(first, count)], pencil.at[pl.ds(first, count), :, here],
            as_sem.at[target], ar_sem.at[me, k], (gx, gy, target))

    end = jnp.logical_or(me == 0, me == nz - 1)

    def send_pair(x, k):
        for d in range(1, nz):
            limit = (me + d < nz, me - d >= 0)
            for toward, inside in zip((me + d, me - d), limit):
                go = inside if d == 1 else jnp.logical_and(inside, jnp.logical_not(end))

                @pl.when(go)
                def _():
                    block(toward, x, 2, k).start()

    def level(read):
        return pooled(read, pairs, rows, work)

    def keep(q, lanes, k, value):
        wide = rows // 2
        for j in range(pairs):
            one[k * pairs + j, q * wide:(q + 1) * wide, lanes] = value[j * wide:(j + 1) * wide, :]

    for k in ORDER:
        for copy in sides[k]:
            copy.wait_recv()
        if k == CHUNKS - 1:
            xcopies[1].wait_recv()
        if k == 0:
            xcopies[0].wait_recv()
        fill = jnp.zeros((LANES - 2 * step, LANES), f32)
        for e in range(2):
            zside[e] = jnp.concatenate([zhalo[e, k], fill], axis=0).T[:cols]

        def pair(i, carry):
            for p in range(2):
                x = k * step + 2 * i + p
                value = magnitude(x, 2 * i + p)
                for q in range(nz):
                    stage[q, x] = value[q * rows:(q + 1) * rows, :]

            @pl.when(i > 0)
            def _():
                send_pair(k * step + 2 * i - 2, k)
            return carry

        lax.fori_loop(0, pairs, pair, 0)

        def own(q, carry):
            piece[q * nz + me, k] = level(lambda p: stage[q, k * step + p])
            return carry

        lax.fori_loop(0, nz, own, 0)
        send_pair((k + 1) * step - 2, k)
        for q in range(nz):
            keep(q, pl.ds(pl.multiple_of(me * half, LANES), half), k, piece[q * nz + me, k])
        for p in range(step):
            pencil[k * step + p, :, pl.ds(pl.multiple_of(me * depth, LANES), depth)] = stage[me, k * step + p]

    def move(j, up, q, s, k):
        here = piece.at[q * nz + s, k]
        return remote(
            here, here, move_sem.at[int(up)], piece_sem.at[q * nz + s, k], (gx, gy, j + 1 if up else j - 1))

    def pass_on(j, q, s, k):
        for up in (True, False):
            came = j not in (q, s) and 0 <= (j + 1 if up else j - 1) < nz and carries(
                nz, j + 1 if up else j - 1, not up, q, s)
            if carries(nz, j, up, q, s) and not came:
                move(j, up, q, s, k).start()

    def rest(j):
        for k in ORDER:
            for q in range(nz):
                pass_on(j, q, j, k)
        if j in (0, nz - 1):
            for k in ORDER:
                for d in range(2, nz):
                    block(d if j == 0 else j - d, k * step, step, k).start()
        for _, q, s, turn in events(nz, j):
            k = ORDER[turn]
            lanes = pl.ds(s * half, half)
            if q == j:
                there = pl.ds(s * depth, depth)
                box = pencil.at[pl.ds(k * step, step), :, there]
                remote(stage.at[s, pl.ds(k * step, step)], box, as_sem.at[s], ar_sem.at[s, k], (gx, gy, s)).wait_recv()
                value = level(lambda p: pencil[k * step + p, :, there])
                piece[q * nz + s, k] = value
                keep(q, lanes, k, value)
                pass_on(j, q, s, k)
            else:
                here = piece.at[q * nz + s, k]
                remote(here, here, move_sem.at[0], piece_sem.at[q * nz + s, k], (gx, gy, (j + 1) % nz)).wait_recv()
                pass_on(j, q, s, k)
                keep(q, lanes, k, piece[q * nz + s, k])
        for up in (True, False):
            count = sum(carries(nz, j, up, q, s) for q, s in blocks(nz))
            if count:
                sent = piece.at[pl.ds(0, count)]
                other = j + 1 if up else j - 1
                remote(sent, sent, move_sem.at[int(up)], piece_sem.at[0, 0], (gx, gy, other)).wait_send()

    for j in range(nz):
        pl.when(me == j)(functools.partial(rest, j))

    for copy in xcopies + [c for k in ORDER for c in sides[k]]:
        copy.wait_send()
    for p in range(nz):
        @pl.when(p != me)
        def _():
            block(p, 0, planes, 0).wait_send()


def finish(pencil_in, one_in, pencil, one, two, three, four, five, two_buf, three_buf, four_buf, a, b, c, d, sem):
    copies = [
        pltpu.make_async_copy(pencil_in, pencil, sem.at[0]),
        pltpu.make_async_copy(one_in, one, sem.at[1]),
    ]
    for copy in copies:
        copy.start()
    source = one_in
    for buf, work, target in (
        (two_buf, a, None), (three_buf, b, three), (four_buf, c, four), (None, d, five)
    ):
        planes, size, _ = source.shape
        planes = planes // 2
        value = pooled(lambda i: source[i], planes, size, work)
        size = size // 2
        if buf is None:
            for j in range(size):
                for i in range(planes):
                    target[j, i:i + 1, :] = value[i * size + j:i * size + j + 1, :]
            break
        for i in range(planes):
            buf[i] = value[i * size:(i + 1) * size, :]
        if target is None:
            copies.append(pltpu.make_async_copy(buf, two, sem.at[2]))
            copies[-1].start()
        else:
            for j in range(size):
                target[j] = buf[:, j, :]
        source = buf
    for copy in copies:
        copy.wait()


def on_device(velocity):
    nx, ny, nz = (lax.axis_size(a) for a in ("gx", "gy", "gz"))
    _, planes, cols, depth = velocity.shape
    full = depth * nz
    step = planes // CHUNKS
    f32 = jnp.float32

    def level(k):
        return jax.ShapeDtypeStruct((planes >> k, cols >> k, full >> k), f32)

    def flipped(k):
        return jax.ShapeDtypeStruct((cols >> k, planes >> k, full >> k), f32)

    def work(lines, depth):
        return pltpu.VMEM((pl.cdiv(depth, LANES), lines, LANES), f32)

    def paired(k):
        return work((planes >> k + 1) * (cols >> k), full >> k)

    vmem = pl.BlockSpec(memory_space=pltpu.VMEM)
    anywhere = pl.BlockSpec(memory_space=pl.ANY)
    dma = pltpu.SemaphoreType.DMA
    first = pl.pallas_call(
        functools.partial(kernel, (nx, ny, nz)),
        out_shape=(jax.ShapeDtypeStruct((planes, cols // nz, full), f32), level(1)),
        in_specs=[pl.BlockSpec(memory_space=pltpu.HBM)],
        out_specs=(vmem, vmem),
        scratch_shapes=[
            pltpu.VMEM((3, planes + 2, cols, depth), f32),
            pltpu.VMEM((2, 2, planes, depth), f32),
            pltpu.VMEM((2, 2, planes, depth), f32),
            pltpu.VMEM((2, CHUNKS, 2 * step, LANES), f32),
            pltpu.VMEM((2, CHUNKS, 2 * step, LANES), f32),
            pltpu.VMEM((2, cols, LANES), f32),
            pltpu.VMEM((nz, planes, cols // nz, depth), f32),
            pltpu.VMEM((nz * nz, CHUNKS, step // 2 * cols // nz // 2, depth // 2), f32),
            work(step // 2 * cols // nz, depth),
            dma((CHUNKS,)), dma((2,)), dma((2,)),
            dma((2, CHUNKS)), dma((2, CHUNKS)), dma((2, CHUNKS)), dma((2, CHUNKS)),
            dma((nz,)), dma((nz, CHUNKS)), dma((2,)), dma((nz * nz, CHUNKS)),
        ],
        compiler_params=pltpu.CompilerParams(
            collective_id=0, has_side_effects=True, vmem_limit_bytes=47 * MIB
        ),
    )(velocity)
    last = pl.pallas_call(
        finish,
        out_shape=tuple(jax.ShapeDtypeStruct(x.shape, f32) for x in first)
        + (level(2), flipped(3), flipped(4), flipped(5)),
        in_specs=[vmem] * 2,
        out_specs=(anywhere,) * 3 + (vmem,) * 3,
        scratch_shapes=[
            *(pltpu.VMEM(level(k).shape, f32) for k in (2, 3, 4)), *(paired(k) for k in (1, 2, 3, 4)), dma((3,))],
        compiler_params=pltpu.CompilerParams(vmem_limit_bytes=8 * MIB),
    )(*first)
    return tuple(last[:3]) + tuple(jnp.transpose(x, (1, 0, 2)) for x in last[3:])


def solution(mesh):
    in_specs = (P(None, "gx", "gy", "gz"),)
    out_specs = (P("gx", ("gy", "gz"), None),) + (P("gx", "gy", None),) * 5
    return jax.shard_map(
        on_device, mesh=mesh, in_specs=in_specs, out_specs=out_specs, check_vma=False
    )
```

profile of v0, /device:TPU:0, one launch (start us, length us, event | category | flops | bytes accessed | tf_op | source)
XLA Modules:
  0.0 106.7 jit_solution(1046659208687755564)
XLA Ops:
  0.6 103.0 %shard_map.62 = (f32[32,24,1024]{2,1,0:T(8,128)S(1)}, f32[16,48,512]{2,1,0:T(8,128)S(1)}) custom-call(f32[3,32,96,256]{3,2,1,0:T(8,128)} %vel_hbm.1), custom_call_target="tpu_custom_call" | custom-call | tf_op jit(solution)/shard_map/pallas_call | solution.py:359
  103.7 3.0 %shard_map.63 = (f32[32,24,1024]{2,1,0:T(8,128)}, f32[16,48,512]{2,1,0:T(8,128)}, f32[8,24,256]{2,1,0:T(8,128)}, f32[12,4,128]{2,1,0:T(4,128)}, f32[6,2,64]{2,1,0:T(2,128)}, /*index=5*/f32[3,1,32]{2,1,0:T(1,128)}) custom-call(f32[32,24,1024]{2,1,0:T(8,128)S(1)} %get-tuple-element.14.pencil_in, f32[16,48,512]{2,1,0:T(8,128)S(1)} %get-tuple-element.15.one_in), custom_call_target="tpu_custom_call" | custom-call | tf_op jit(solution)/shard_map/pallas_call | solution.py:382
where the time goes:
time: 107 us
  Pallas kernels  106 us (99%)
    pallas_call x1, Pallas kernels, on_device(): pl.pallas_call(functools.partial(kernel, (nx, ny, nz)), out_shape=(jax.Sh...  103 us
    pallas_call x1, Pallas kernels, on_device(): pl.pallas_call(finish, out_shape=tuple((jax.ShapeDtypeStruct(x.shape, f32...  3.03 us

commit v1 on v0

--- a/solution.py
+++ b/solution.py
@@ -51,50 +51,49 @@
     return halve_lanes(jnp.concatenate(parts, axis=1)[:, :depth])
 
 
-def carries(n, j, up, q, s):
-    low, high = min(q, s), max(q, s)
-    if up:
-        return j < n - 1 and (high <= j or (low <= j and high > j + 1 and 2 * (j + 1) < n))
-    return j > 0 and (low >= j or (high >= j and low < j - 1 and 2 * (j - 1) >= n))
-
-
-def blocks(n):
-    return [(q, s) for q in range(n) for s in range(n)]
-
-
-def mag_time(n, s, q, k):
-    d = abs(s - q)
-    if s in (0, n - 1):
-        return 4 * (k + 1) if d == 1 else 20 + 14 * (k + (d - 1) / (n - 2))
-    outward = q < s if 2 * s < n else q > s
-    return 4 * k + 6 if outward else 12 * (k + d / n)
-
-
-def events(n, me):
-    @functools.lru_cache(None)
-    def ready(j, q, s, k):
-        if j == s:
-            return 0.0
-        if j == q:
-            return mag_time(n, s, q, k)
-        for i, up in ((j - 1, True), (j + 1, False)):
-            if 0 <= i < n and carries(n, i, up, q, s):
-                crossing = 2 * (i + 1) == n if up else 2 * i == n
-                return max(ready(i, q, s, k), (50 if crossing else 20) + 2 * k) + 3
-        raise ValueError((j, q, s))
-
-    found = []
-    for k in range(CHUNKS):
-        for q, s in blocks(n):
-            if s != me:
-                found.append((ready(me, q, s, k), q, s, k))
-    return sorted(found)
+def arrivals(n):
+    coming = [[]]
+    small = 0.5 / CHUNKS
+    for j in range(n - 1):
+        sends = []
+        for k in range(CHUNKS):
+            sends.append((2.5 * k, 1.0, (True, j, n - 1, k)))
+            sends += [(2.5 * k + 2.0, small, (False, j, q, k)) for q in range(j + 1)]
+        between = [(True, j, q, k) for q in range(j + 1, n - 1) for k in range(CHUNKS)]
+        relays = [i for i, (_, (mags, _, q, _)) in enumerate(coming[j]) if mags and q == n - 1]
+        if not relays:
+            sends += [(10.0, 1.0, item) for item in between]
+        for i, (time, (mags, s, q, k)) in enumerate(coming[j]):
+            time = max(time, 10.0)
+            sends.append((time, 1.0 if mags and q != j else small, (mags and q != j, s, q, k)))
+            if relays and i == relays[-1]:
+                sends += [(time, 1.0, item) for item in between]
+        now, there = 0.0, []
+        for ready, size, item in sends:
+            now = max(now, ready) + 4.2 * size
+            there.append((now + 2.0, item))
+        coming.append(there)
+    return coming
+
+
+def schedule(n, j):
+    coming = arrivals(n)
+    events = [(time, True) + item for time, item in coming[j]]
+    for time, (mags, s, q, k) in coming[n - 1 - j]:
+        events.append((time, False, mags, n - 1 - s, n - 1 - q, k))
+    return [e[1:] for e in sorted(events, key=lambda e: e[0])]
+
+
+def slots(n, j):
+    pairs = [(s, q) for s in range(j) for q in range(j + 1, n)]
+    pairs += [(s, q) for s in range(j + 1, n) for q in range(j)]
+    return {pair: i for i, pair in enumerate(pairs)}
 
 
 def kernel(
     sizes, vel_hbm, pencil, one,
-    vel, ypack, yhalo, zpack, zhalo, zside, stage, piece, work,
-    load_sem, xs_sem, xr_sem, ys_sem, yr_sem, zs_sem, zr_sem, as_sem, ar_sem, move_sem, piece_sem,
+    vel, ypack, yhalo, zpack, zhalo, zside, stage, transit, piece, work,
+    load_sem, xs_sem, xr_sem, ys_sem, yr_sem, zs_sem, zr_sem, mag_sem, ar_sem, tr_sem, move_sem, piece_sem,
 ):
     nx, ny, nz = sizes
     gx, gy, me = lax.axis_index("gx"), lax.axis_index("gy"), lax.axis_index("gz")
@@ -185,23 +184,28 @@
         total = total + part * part
         return jnp.sqrt(1.0 + 0.25 * total)
 
-    def block(target, first, count, k):
-        here = pl.ds(pl.multiple_of(me * depth, LANES), depth)
-        return remote(
-            stage.at[target, pl.ds(first, count)], pencil.at[pl.ds(first, count), :, here],
-            as_sem.at[target], ar_sem.at[me, k], (gx, gy, target))
-
-    end = jnp.logical_or(me == 0, me == nz - 1)
+    def landing(j, s, q, where):
+        if q == j:
+            return pencil.at[where, :, pl.ds(s * depth, depth)]
+        return transit.at[slots(nz, j)[s, q], where]
 
     def send_pair(x, k):
-        for d in range(1, nz):
-            limit = (me + d < nz, me - d >= 0)
-            for toward, inside in zip((me + d, me - d), limit):
-                go = inside if d == 1 else jnp.logical_and(inside, jnp.logical_not(end))
-
-                @pl.when(go)
-                def _():
-                    block(toward, x, 2, k).start()
+        where = pl.ds(x, 2)
+        own = pl.ds(pl.multiple_of(me * depth, LANES), depth)
+        for up in (True, False):
+            target = nz - 1 if up else 0
+            other = me + 1 if up else me - 1
+            slot = me * (nz - 2 - me) + nz - 3 - me if up else (me - 1) * (nz - me)
+
+            @pl.when(jnp.logical_and(other == target, me != target))
+            def _():
+                remote(stage.at[target, where], pencil.at[where, :, own],
+                       mag_sem.at[int(up), 0], ar_sem.at[me, k], (gx, gy, other)).start()
+
+            @pl.when(jnp.logical_and(other != target, me != target))
+            def _():
+                remote(stage.at[target, where], transit.at[slot, where],
+                       mag_sem.at[int(up), 0], tr_sem.at[slot, k], (gx, gy, other)).start()
 
     def level(read):
         return pooled(read, pairs, rows, work)
@@ -210,6 +214,11 @@
         wide = rows // 2
         for j in range(pairs):
             one[k * pairs + j, q * wide:(q + 1) * wide, lanes] = value[j * wide:(j + 1) * wide, :]
+
+    def move(j, up, q, s, k):
+        here = piece.at[q * nz + s, k]
+        return remote(
+            here, here, move_sem.at[int(up)], piece_sem.at[q * nz + s, k], (gx, gy, j + 1 if up else j - 1))
 
     for k in ORDER:
         for copy in sides[k]:
@@ -246,59 +255,84 @@
             keep(q, pl.ds(pl.multiple_of(me * half, LANES), half), k, piece[q * nz + me, k])
         for p in range(step):
             pencil[k * step + p, :, pl.ds(pl.multiple_of(me * depth, LANES), depth)] = stage[me, k * step + p]
-
-    def move(j, up, q, s, k):
-        here = piece.at[q * nz + s, k]
-        return remote(
-            here, here, move_sem.at[int(up)], piece_sem.at[q * nz + s, k], (gx, gy, j + 1 if up else j - 1))
-
-    def pass_on(j, q, s, k):
+        for q in range(nz):
+            @pl.when(jnp.logical_and(me < nz - 1, me >= q))
+            def _():
+                move(me, True, q, me, k).start()
+
+            @pl.when(jnp.logical_and(me > 0, me <= q))
+            def _():
+                move(me, False, q, me, k).start()
+
+    def rest(j):
+        sent = ({}, {})
+
+        def mags(up, s, q, turn):
+            k = ORDER[turn]
+            where = pl.ds(k * step, step)
+            other = j + 1 if up else j - 1
+            source = stage.at[q, where] if s == j else transit.at[slots(nz, j)[s, q], where]
+            arrived = ar_sem.at[s, k] if q == other else tr_sem.at[slots(nz, other)[s, q], k]
+            row = sent[up].setdefault((s, q), len(sent[up]))
+            return remote(source, landing(other, s, q, where), mag_sem.at[int(up), row], arrived, (gx, gy, other))
+
+        def between(up):
+            for q in range(j + 1, nz - 1) if up else reversed(range(1, j)):
+                for turn in range(CHUNKS):
+                    mags(up, j, q, turn).start()
+
+        events = schedule(nz, j)
+        last = {}
+        for up, far in ((True, nz - 1), (False, 0)):
+            if j != far:
+                sent[up][j, far] = 0
+                waiting = [i for i, (e, whole, _, q, _) in enumerate(events) if e == up and whole and q == far]
+                if waiting:
+                    last[waiting[-1]] = up
+                else:
+                    between(up)
+        for i, (up, whole, s, q, turn) in enumerate(events):
+            k = ORDER[turn]
+            more = j < nz - 1 if up else j > 0
+            before = (gx, gy, j - 1 if up else j + 1)
+            here = piece.at[q * nz + s, k]
+            if whole:
+                where = pl.ds(k * step, step)
+                box = landing(j, s, q, where)
+                arrived = ar_sem.at[s, k] if q == j else tr_sem.at[slots(nz, j)[s, q], k]
+                remote(box, box, mag_sem.at[0, 0], arrived, before).wait_recv()
+                if q != j:
+                    mags(up, s, q, turn).start()
+                    slot = slots(nz, j)[s, q]
+                    value = level(lambda p: transit[slot, k * step + p])
+                else:
+                    value = level(lambda p: pencil[k * step + p, :, pl.ds(s * depth, depth)])
+                    if more:
+                        piece[q * nz + s, k] = value
+            else:
+                remote(here, here, move_sem.at[0], piece_sem.at[q * nz + s, k], before).wait_recv()
+                if more:
+                    move(j, up, q, s, k).start()
+                value = piece[q * nz + s, k]
+            keep(q, pl.ds(s * half, half), k, value)
+            if whole and q == j and more:
+                move(j, up, q, s, k).start()
+            if i in last:
+                between(last[i])
         for up in (True, False):
-            came = j not in (q, s) and 0 <= (j + 1 if up else j - 1) < nz and carries(
-                nz, j + 1 if up else j - 1, not up, q, s)
-            if carries(nz, j, up, q, s) and not came:
-                move(j, up, q, s, k).start()
-
-    def rest(j):
-        for k in ORDER:
-            for q in range(nz):
-                pass_on(j, q, j, k)
-        if j in (0, nz - 1):
-            for k in ORDER:
-                for d in range(2, nz):
-                    block(d if j == 0 else j - d, k * step, step, k).start()
-        for _, q, s, turn in events(nz, j):
-            k = ORDER[turn]
-            lanes = pl.ds(s * half, half)
-            if q == j:
-                there = pl.ds(s * depth, depth)
-                box = pencil.at[pl.ds(k * step, step), :, there]
-                remote(stage.at[s, pl.ds(k * step, step)], box, as_sem.at[s], ar_sem.at[s, k], (gx, gy, s)).wait_recv()
-                value = level(lambda p: pencil[k * step + p, :, there])
-                piece[q * nz + s, k] = value
-                keep(q, lanes, k, value)
-                pass_on(j, q, s, k)
-            else:
-                here = piece.at[q * nz + s, k]
-                remote(here, here, move_sem.at[0], piece_sem.at[q * nz + s, k], (gx, gy, (j + 1) % nz)).wait_recv()
-                pass_on(j, q, s, k)
-                keep(q, lanes, k, piece[q * nz + s, k])
-        for up in (True, False):
-            count = sum(carries(nz, j, up, q, s) for q, s in blocks(nz))
-            if count:
-                sent = piece.at[pl.ds(0, count)]
-                other = j + 1 if up else j - 1
-                remote(sent, sent, move_sem.at[int(up)], piece_sem.at[0, 0], (gx, gy, other)).wait_send()
+            other = (gx, gy, j + 1 if up else j - 1)
+            for row in sent[up].values():
+                remote(stage.at[0], stage.at[0], mag_sem.at[int(up), row], ar_sem.at[0, 0], other).wait_send()
+            count = (j + 1) ** 2 if up else (nz - j) ** 2
+            if j != (nz - 1 if up else 0):
+                moved = piece.at[pl.ds(0, count)]
+                remote(moved, moved, move_sem.at[int(up)], piece_sem.at[0, 0], other).wait_send()
 
     for j in range(nz):
         pl.when(me == j)(functools.partial(rest, j))
 
     for copy in xcopies + [c for k in ORDER for c in sides[k]]:
         copy.wait_send()
-    for p in range(nz):
-        @pl.when(p != me)
-        def _():
-            block(p, 0, planes, 0).wait_send()
 
 
 def finish(pencil_in, one_in, pencil, one, two, three, four, five, two_buf, three_buf, four_buf, a, b, c, d, sem):
@@ -339,6 +373,8 @@
     _, planes, cols, depth = velocity.shape
     full = depth * nz
     step = planes // CHUNKS
+    relayed = max(1, *(len(slots(nz, j)) for j in range(nz)))
+    passing = max((j + 1) * (nz - 1 - j) for j in range(nz))
     f32 = jnp.float32
 
     def level(k):
@@ -369,11 +405,12 @@
             pltpu.VMEM((2, CHUNKS, 2 * step, LANES), f32),
             pltpu.VMEM((2, cols, LANES), f32),
             pltpu.VMEM((nz, planes, cols // nz, depth), f32),
+            pltpu.VMEM((relayed, planes, cols // nz, depth), f32),
             pltpu.VMEM((nz * nz, CHUNKS, step // 2 * cols // nz // 2, depth // 2), f32),
             work(step // 2 * cols // nz, depth),
             dma((CHUNKS,)), dma((2,)), dma((2,)),
             dma((2, CHUNKS)), dma((2, CHUNKS)), dma((2, CHUNKS)), dma((2, CHUNKS)),
-            dma((nz,)), dma((nz, CHUNKS)), dma((2,)), dma((nz * nz, CHUNKS)),
+            dma((2, passing)), dma((nz, CHUNKS)), dma((relayed, CHUNKS)), dma((2,)), dma((nz * nz, CHUNKS)),
         ],
         compiler_params=pltpu.CompilerParams(
             collective_id=0, has_side_effects=True, vmem_limit_bytes=47 * MIB

time: 107 us -> 95.5 us (0.89)
  Pallas kernels: 106 us -> 94.7 us
    pallas_call x1, Pallas kernels: 103 us -> 91.6 us  [on_device(): pl.pallas_call(functools.partial(kernel, (nx, ny, nz)), out_shape=(jax.Sh...]
where the time goes in v1:
time: 95.5 us; the launch traced here: 95.3 us
  Pallas kernels  94.7 us (99%)
    pallas_call x1, Pallas kernels, on_device(): pl.pallas_call(functools.partial(kernel, (nx, ny, nz)), out_shape=(jax.Sh...  91.6 us
    pallas_call x1, Pallas kernels, on_device(): pl.pallas_call(finish, out_shape=tuple((jax.ShapeDtypeStruct(x.shape, f32...  3.03 us

profile of v1, /device:TPU:0, one launch (start us, length us, event | category | flops | bytes accessed | tf_op | source)
XLA Modules:
  0.0 95.3 jit_solution(1801169659234604172)
XLA Ops:
  0.6 91.6 %shard_map.62 = (f32[32,24,1024]{2,1,0:T(8,128)S(1)}, f32[16,48,512]{2,1,0:T(8,128)S(1)}) custom-call(f32[3,32,96,256]{3,2,1,0:T(8,128)} %vel_hbm.1), custom_call_target="tpu_custom_call" | custom-call | tf_op jit(solution)/shard_map/pallas_call | solution.py:395
  92.3 3.0 %shard_map.63 = (f32[32,24,1024]{2,1,0:T(8,128)}, f32[16,48,512]{2,1,0:T(8,128)}, f32[8,24,256]{2,1,0:T(8,128)}, f32[12,4,128]{2,1,0:T(4,128)}, f32[6,2,64]{2,1,0:T(2,128)}, /*index=5*/f32[3,1,32]{2,1,0:T(1,128)}) custom-call(f32[32,24,1024]{2,1,0:T(8,128)S(1)} %get-tuple-element.14.pencil_in, f32[16,48,512]{2,1,0:T(8,128)S(1)} %get-tuple-element.15.one_in), custom_call_target="tpu_custom_call" | custom-call | tf_op jit(solution)/shard_map/pallas_call | solution.py:419

commit v2 on v1

--- a/solution.py
+++ b/solution.py
@@ -49,6 +49,10 @@
     parts = [
         work[t, pl.ds(0, lines, stride=2), :] + work[t, pl.ds(1, lines, stride=2), :] for t in range(tiles)]
     return halve_lanes(jnp.concatenate(parts, axis=1)[:, :depth])
+
+
+def ahead(n, s, q, k):
+    return k == CHUNKS - 1 and abs(q - s) > 1 and 0 < q < n - 1
 
 
 def arrivals(n):
@@ -65,7 +69,10 @@
             sends += [(10.0, 1.0, item) for item in between]
         for i, (time, (mags, s, q, k)) in enumerate(coming[j]):
             time = max(time, 10.0)
-            sends.append((time, 1.0 if mags and q != j else small, (mags and q != j, s, q, k)))
+            if mags and q == j + 1 and ahead(n, s, q, k):
+                sends.append((time, small, (False, s, q, k)))
+            if not mags or q != j or not ahead(n, s, q, k):
+                sends.append((time, 1.0 if mags and q != j else small, (mags and q != j, s, q, k)))
             if relays and i == relays[-1]:
                 sends += [(time, 1.0, item) for item in between]
         now, there = 0.0, []
@@ -109,7 +116,7 @@
         return (lax.rem(gx + dx + nx, nx), lax.rem(gy + dy + ny, ny), lax.rem(me + dz + nz, nz))
 
     barrier = pltpu.get_barrier_semaphore()
-    friends = [at(dx=1), at(dx=-1), at(dy=1), at(dy=-1)] + [at(dz=d) for d in range(1, nz)]
+    friends = [at(dx=1), at(dx=-1), at(dy=1), at(dy=-1), at(dz=1), at(dz=-1)]
     for friend in friends:
         pl.semaphore_signal(barrier, inc=1, device_id=friend, device_id_type=MESH)
 
@@ -118,15 +125,10 @@
         loads[k] = pltpu.make_async_copy(
             vel_hbm.at[:, pl.ds(k * step, step)], vel.at[:, pl.ds(1 + k * step, step)], load_sem.at[k])
         loads[k].start()
-    pl.semaphore_wait(barrier, len(friends))
-
     xcopies = [
         remote(vel_hbm.at[pl.ds(1, 2), planes - 1], vel.at[pl.ds(1, 2), 0], xs_sem.at[0], xr_sem.at[0], at(dx=1)),
         remote(vel_hbm.at[pl.ds(1, 2), 0], vel.at[pl.ds(1, 2), planes + 1], xs_sem.at[1], xr_sem.at[1], at(dx=-1)),
     ]
-    for copy in xcopies:
-        copy.start()
-
     lane = lax.broadcasted_iota(jnp.int32, (cols, LANES), 1)
     sides = {}
     for k in ORDER:
@@ -146,6 +148,8 @@
         fill = jnp.zeros((LANES - cols, LANES), f32)
         for e in range(2):
             zpack[e, k] = jnp.concatenate([ends[e], fill], axis=0).T[:2 * step]
+        if k == ORDER[0]:
+            pl.semaphore_wait(barrier, len(friends))
         mine = pl.ds(k * step, step)
         sides[k] = [
             remote(ypack.at[1, :, mine], yhalo.at[0, :, mine], ys_sem.at[0, k], yr_sem.at[0, k], at(dy=1)),
@@ -153,7 +157,7 @@
             remote(zpack.at[1, k], zhalo.at[0, k], zs_sem.at[0, k], zr_sem.at[0, k], at(dz=1)),
             remote(zpack.at[0, k], zhalo.at[1, k], zs_sem.at[1, k], zr_sem.at[1, k], at(dz=-1)),
         ]
-        for copy in sides[k]:
+        for copy in sides[k] + (xcopies if k == ORDER[0] else []):
             copy.start()
 
     row = lax.broadcasted_iota(jnp.int32, (cols, depth), 0)
@@ -207,6 +211,9 @@
                 remote(stage.at[target, where], transit.at[slot, where],
                        mag_sem.at[int(up), 0], tr_sem.at[slot, k], (gx, gy, other)).start()
 
+    def at_piece(q, s, k):
+        return (q * nz + s) * CHUNKS + k
+
     def level(read):
         return pooled(read, pairs, rows, work)
 
@@ -216,7 +223,7 @@
             one[k * pairs + j, q * wide:(q + 1) * wide, lanes] = value[j * wide:(j + 1) * wide, :]
 
     def move(j, up, q, s, k):
-        here = piece.at[q * nz + s, k]
+        here = piece.at[at_piece(q, s, k)]
         return remote(
             here, here, move_sem.at[int(up)], piece_sem.at[q * nz + s, k], (gx, gy, j + 1 if up else j - 1))
 
@@ -246,13 +253,13 @@
         lax.fori_loop(0, pairs, pair, 0)
 
         def own(q, carry):
-            piece[q * nz + me, k] = level(lambda p: stage[q, k * step + p])
+            piece[at_piece(q, me, k)] = level(lambda p: stage[q, k * step + p])
             return carry
 
         lax.fori_loop(0, nz, own, 0)
         send_pair((k + 1) * step - 2, k)
         for q in range(nz):
-            keep(q, pl.ds(pl.multiple_of(me * half, LANES), half), k, piece[q * nz + me, k])
+            keep(q, pl.ds(pl.multiple_of(me * half, LANES), half), k, piece[at_piece(q, me, k)])
         for p in range(step):
             pencil[k * step + p, :, pl.ds(pl.multiple_of(me * depth, LANES), depth)] = stage[me, k * step + p]
         for q in range(nz):
@@ -291,29 +298,41 @@
                     last[waiting[-1]] = up
                 else:
                     between(up)
+        extra = [0, 0]
         for i, (up, whole, s, q, turn) in enumerate(events):
             k = ORDER[turn]
             more = j < nz - 1 if up else j > 0
             before = (gx, gy, j - 1 if up else j + 1)
-            here = piece.at[q * nz + s, k]
+            here = piece.at[at_piece(q, s, k)]
             if whole:
                 where = pl.ds(k * step, step)
                 box = landing(j, s, q, where)
                 arrived = ar_sem.at[s, k] if q == j else tr_sem.at[slots(nz, j)[s, q], k]
                 remote(box, box, mag_sem.at[0, 0], arrived, before).wait_recv()
                 if q != j:
-                    mags(up, s, q, turn).start()
                     slot = slots(nz, j)[s, q]
+                    first = q == (j + 1 if up else j - 1) and ahead(nz, s, q, turn)
+                    if not first:
+                        mags(up, s, q, turn).start()
                     value = level(lambda p: transit[slot, k * step + p])
+                    if first:
+                        piece[at_piece(q, s, k)] = value
+                        keep(q, pl.ds(s * half, half), k, value)
+                        move(j, up, q, s, k).start()
+                        mags(up, s, q, turn).start()
+                        extra[up] += 1
+                        continue
+                elif ahead(nz, s, q, turn):
+                    continue
                 else:
                     value = level(lambda p: pencil[k * step + p, :, pl.ds(s * depth, depth)])
                     if more:
-                        piece[q * nz + s, k] = value
+                        piece[at_piece(q, s, k)] = value
             else:
                 remote(here, here, move_sem.at[0], piece_sem.at[q * nz + s, k], before).wait_recv()
                 if more:
                     move(j, up, q, s, k).start()
-                value = piece[q * nz + s, k]
+                value = piece[at_piece(q, s, k)]
             keep(q, pl.ds(s * half, half), k, value)
             if whole and q == j and more:
                 move(j, up, q, s, k).start()
@@ -323,7 +342,7 @@
             other = (gx, gy, j + 1 if up else j - 1)
             for row in sent[up].values():
                 remote(stage.at[0], stage.at[0], mag_sem.at[int(up), row], ar_sem.at[0, 0], other).wait_send()
-            count = (j + 1) ** 2 if up else (nz - j) ** 2
+            count = ((j + 1) ** 2 if up else (nz - j) ** 2) * CHUNKS + extra[up]
             if j != (nz - 1 if up else 0):
                 moved = piece.at[pl.ds(0, count)]
                 remote(moved, moved, move_sem.at[int(up)], piece_sem.at[0, 0], other).wait_send()
@@ -406,7 +425,7 @@
             pltpu.VMEM((2, cols, LANES), f32),
             pltpu.VMEM((nz, planes, cols // nz, depth), f32),
             pltpu.VMEM((relayed, planes, cols // nz, depth), f32),
-            pltpu.VMEM((nz * nz, CHUNKS, step // 2 * cols // nz // 2, depth // 2), f32),
+            pltpu.VMEM((nz * nz * CHUNKS, step // 2 * cols // nz // 2, depth // 2), f32),
             work(step // 2 * cols // nz, depth),
             dma((CHUNKS,)), dma((2,)), dma((2,)),
             dma((2, CHUNKS)), dma((2, CHUNKS)), dma((2, CHUNKS)), dma((2, CHUNKS)),

time: 95.5 us -> 92.7 us (0.971)
  Pallas kernels: 94.7 us -> 91.9 us
    pallas_call x1, Pallas kernels: 91.6 us -> 88.9 us  [on_device(): pl.pallas_call(functools.partial(kernel, (nx, ny, nz)), out_shape=(jax.Sh...]
where the time goes in v2:
time: 92.7 us; the launch traced here: 92.5 us
  Pallas kernels  91.9 us (99%)
    pallas_call x1, Pallas kernels, on_device(): pl.pallas_call(functools.partial(kernel, (nx, ny, nz)), out_shape=(jax.Sh...  88.9 us
    pallas_call x1, Pallas kernels, on_device(): pl.pallas_call(finish, out_shape=tuple((jax.ShapeDtypeStruct(x.shape, f32...  3.03 us

profile of v2, /device:TPU:0, one launch (start us, length us, event | category | flops | bytes accessed | tf_op | source)
XLA Modules:
  0.0 92.5 jit_solution(16516565033377945827)
XLA Ops:
  0.6 88.9 %shard_map.62 = (f32[32,24,1024]{2,1,0:T(8,128)S(1)}, f32[16,48,512]{2,1,0:T(8,128)S(1)}) custom-call(f32[3,32,96,256]{3,2,1,0:T(8,128)} %vel_hbm.1), custom_call_target="tpu_custom_call" | custom-call | tf_op jit(solution)/shard_map/pallas_call | solution.py:414
  89.5 3.0 %shard_map.63 = (f32[32,24,1024]{2,1,0:T(8,128)}, f32[16,48,512]{2,1,0:T(8,128)}, f32[8,24,256]{2,1,0:T(8,128)}, f32[12,4,128]{2,1,0:T(4,128)}, f32[6,2,64]{2,1,0:T(2,128)}, /*index=5*/f32[3,1,32]{2,1,0:T(1,128)}) custom-call(f32[32,24,1024]{2,1,0:T(8,128)S(1)} %get-tuple-element.14.pencil_in, f32[16,48,512]{2,1,0:T(8,128)S(1)} %get-tuple-element.15.one_in), custom_call_target="tpu_custom_call" | custom-call | tf_op jit(solution)/shard_map/pallas_call | solution.py:438

commit v3 on v2

--- a/solution.py
+++ b/solution.py
@@ -52,7 +52,7 @@
 
 
 def ahead(n, s, q, k):
-    return k == CHUNKS - 1 and abs(q - s) > 1 and 0 < q < n - 1
+    return k >= CHUNKS - 2 and abs(q - s) > 1 and 0 < q < n - 1
 
 
 def arrivals(n):
@@ -71,7 +71,9 @@
             time = max(time, 10.0)
             if mags and q == j + 1 and ahead(n, s, q, k):
                 sends.append((time, small, (False, s, q, k)))
-            if not mags or q != j or not ahead(n, s, q, k):
+                if k == CHUNKS - 1:
+                    sends += [(time, 1.0, (True, s, q, held)) for held in (k - 1, k)]
+            elif not mags or q != j or not ahead(n, s, q, k):
                 sends.append((time, 1.0 if mags and q != j else small, (mags and q != j, s, q, k)))
             if relays and i == relays[-1]:
                 sends += [(time, 1.0, item) for item in between]
@@ -319,7 +321,9 @@
                         piece[at_piece(q, s, k)] = value
                         keep(q, pl.ds(s * half, half), k, value)
                         move(j, up, q, s, k).start()
-                        mags(up, s, q, turn).start()
+                        if turn == CHUNKS - 1:
+                            mags(up, s, q, turn - 1).start()
+                            mags(up, s, q, turn).start()
                         extra[up] += 1
                         continue
                 elif ahead(nz, s, q, turn):

time: 92.7 us -> 91.4 us (0.986)
  the two profiles are of different devices: /device:TPU:0 before, /device:TPU:10 now
where the time goes in v3:
time: 91.4 us; the launch traced here: 91.3 us
  Pallas kernels  90.7 us (99%)
    pallas_call x1, Pallas kernels, on_device(): pl.pallas_call(functools.partial(kernel, (nx, ny, nz)), out_shape=(jax.Sh...  87.6 us
    pallas_call x1, Pallas kernels, on_device(): pl.pallas_call(finish, out_shape=tuple((jax.ShapeDtypeStruct(x.shape, f32...  3.03 us

profile of v3, /device:TPU:10, one launch (start us, length us, event | category | flops | bytes accessed | tf_op | source)
XLA Modules:
  0.0 91.3 jit_solution(6484143222586549626)
XLA Ops:
  0.6 87.6 %shard_map.62 = (f32[32,24,1024]{2,1,0:T(8,128)S(1)}, f32[16,48,512]{2,1,0:T(8,128)S(1)}) custom-call(f32[3,32,96,256]{3,2,1,0:T(8,128)} %vel_hbm.1), custom_call_target="tpu_custom_call" | custom-call | tf_op jit(solution)/shard_map/pallas_call | solution.py:418
  88.3 3.0 %shard_map.63 = (f32[32,24,1024]{2,1,0:T(8,128)}, f32[16,48,512]{2,1,0:T(8,128)}, f32[8,24,256]{2,1,0:T(8,128)}, f32[12,4,128]{2,1,0:T(4,128)}, f32[6,2,64]{2,1,0:T(2,128)}, /*index=5*/f32[3,1,32]{2,1,0:T(1,128)}) custom-call(f32[32,24,1024]{2,1,0:T(8,128)S(1)} %get-tuple-element.14.pencil_in, f32[16,48,512]{2,1,0:T(8,128)S(1)} %get-tuple-element.15.one_in), custom_call_target="tpu_custom_call" | custom-call | tf_op jit(solution)/shard_map/pallas_call | solution.py:442
